TPU v7x, 256 devices: a whole 4x4x8 slice. The times are simulated.
256 devices in a mesh: row: 16 (over y, x), col: 16 (over z, core).
Axes of the slice: x: 4, y: 4, z: 8, core: 2. Of those that a mesh axis runs over, the one named last changes fastest.
Arguments:
- trail: float32 [2, 16, 512, 2, 16, 512], P(None, 'row', None, None, 'col'), may hold values from -6 to 6
- panel: float32 [2, 16, 512, 512], P(None, 'row', None, 'col'), may hold values from -6 to 6
- row_basis: float32 [2, 16, 64, 512], P(None, 'row', None, 'col'), may hold values from -0.75 to 0.75
- row_coeff: float32 [2, 16, 64, 512], P(None, 'row', None, 'col'), may hold values from -0.25 to 0.25
- col_basis: float32 [2, 16, 64, 512], P(None, 'col', None, 'row'), may hold values from -0.75 to 0.75
- col_scaled: float32 [2, 16, 64, 512], P(None, 'col', None, 'row'), may hold values from -0.25 to 0.25
- pivot_basis: float32 [64, 512], P(None, 'col'), may hold values from -0.75 to 0.75
- pivot_scaled: float32 [64, 512], replicated, may hold values from -0.25 to 0.25
- sketch: float32 [64, 512], replicated, may hold values from -6 to 6
- perm: int32 [512], replicated, may hold values from 0 to 511, each once
- pair_kind: int32 [256], replicated, may hold values from 0 to 1
- pivot_values: float32 [3, 256], replicated, may hold values from -3 to 3, as said below
Outputs:
- trail_out: float32 [2, 16, 512, 2, 16, 512], P(None, 'row', None, None, 'col')
- basis_out: float32 [2, 16, 64, 512], P(None, 'row')
- coeff_out: float32 [2, 16, 64, 512], P(None, 'row')
Inputs may be any that keep to these rules, and one draw needn't show every extreme that they name: `pivot_values`: rows 0 and 1 have magnitudes between 0.5 and 0.7; row 2 has magnitude 1.2 or more.
All inputs are finite; a program needn't handle non-finite values.
Results may differ from a plain program's by a relative error of at most 0.00013.
Values sent between devices are 32-bit elements; how exact they have to be, the bound alone decides.
A program may use at most 64 MiB of HBM per device.

v0:
```python
import jax
import jax.numpy as jnp
from jax import lax
from jax.sharding import PartitionSpec as P


def gather_turned(arrays, axis, dims):
    turned = [jnp.moveaxis(a, dim, 0) for a, dim in zip(arrays, dims)]
    both = jnp.concatenate([t.reshape(len(t), -1) for t in turned], axis=1)
    filled, at, outs = (lax.all_gather(both, axis, axis=0, tiled=True), 0, [])
    for t, dim in zip(turned, dims):
        share = filled[:, at : at + t[0].size].reshape(-1, *t.shape[1:])
        outs.append(jnp.moveaxis(share, 0, dim))
        at += t[0].size
    return tuple(outs)


def total_of_pieces(array, axis):
    return lax.all_gather(array, axis).sum(0)


def pair_apply(rows, pair_kind, pivot_values):
    shaped = rows.reshape(rows.shape[:-1] + (rows.shape[-1] // 2, 2))
    first_in = shaped[..., 0]
    second_in = shaped[..., 1]
    diag_one = pivot_values[0]
    diag_two = pivot_values[1]
    offdiag = pivot_values[2]
    determinant = diag_one * diag_two - offdiag * offdiag
    twin = pair_kind == 1
    first = jnp.where(
        twin, (first_in * diag_two - second_in * offdiag) / determinant, first_in / diag_one
    )
    second = jnp.where(
        twin, (second_in * diag_one - first_in * offdiag) / determinant, second_in / diag_two
    )
    return jnp.stack([first, second], axis=-1).reshape(rows.shape)


def tri_solve(lower, rhs):
    return jax.vmap(lambda low, right: jax.scipy.linalg.solve_triangular(low, right, lower=True))(
        lower, rhs
    )


def body(
    trail,
    panel,
    row_basis,
    row_coeff,
    col_basis,
    col_scaled,
    pivot_basis,
    pivot_scaled,
    sketch,
    perm,
    pair_kind,
    pivot_values,
):
    highest = lax.Precision.HIGHEST
    width = sketch.shape[1]
    block = panel.shape[3]
    xrows, yrows = gather_turned((row_basis, row_coeff), "col", (3, 3))
    zcols, gcols = gather_turned((col_basis, col_scaled), "row", (3, 3))
    xrows = xrows[:, 0]
    yrows = yrows[:, 0]
    zcols = zcols[:, 0]
    gcols = gcols[:, 0]
    core = jnp.einsum("arp,bsp->arbs", yrows, gcols, precision=highest)
    left = jnp.einsum("arp,arbs->apbs", xrows, core, precision=highest)
    change = jnp.einsum("apbs,bsq->apbq", left, zcols, precision=highest)
    trail_out = trail - change[:, None, :, :, None, :]
    pcore = jnp.einsum("arp,sp->ars", yrows, pivot_scaled, precision=highest)
    pleft = jnp.einsum("arp,ars->aps", xrows, pcore, precision=highest)
    updated = panel[:, 0] - jnp.einsum("aps,sq->apq", pleft, pivot_basis, precision=highest)
    scaled_t = pair_apply(sketch, pair_kind, pivot_values)
    column_ids = lax.axis_index("col") * block + jnp.arange(block, dtype=jnp.int32)
    selector = (perm[:, None] == column_ids[None, :]).astype(jnp.float32)
    local_sketch = jnp.dot(scaled_t, selector, precision=highest)
    partial_range = jnp.einsum("apq,rq->arp", updated, local_sketch, precision=highest)
    range_t = total_of_pieces(partial_range, "col")
    gram = jnp.einsum("arp,asp->ars", range_t, range_t, precision=highest) / width
    basis = tri_solve(jnp.linalg.cholesky(gram), range_t)
    projected_part = jnp.einsum("arp,apq->arq", basis, updated, precision=highest)
    projected = lax.all_gather(projected_part, "col", axis=2, tiled=True)
    permuted = jnp.take(projected, perm, axis=2)
    coeff = pair_apply(permuted, pair_kind, pivot_values) / jnp.sqrt(jnp.float32(width))
    return (trail_out, basis[:, None], coeff[:, None])


def solution(mesh):
    return jax.shard_map(
        body,
        mesh=mesh,
        in_specs=(
            P(None, "row", None, None, "col", None),
            P(None, "row", None, "col"),
            P(None, "row", None, "col"),
            P(None, "row", None, "col"),
            P(None, "col", None, "row"),
            P(None, "col", None, "row"),
            P(None, "col"),
            P(),
            P(),
            P(),
            P(),
            P(),
        ),
        out_specs=(
            P(None, "row", None, None, "col", None),
            P(None, "row", None, None),
            P(None, "row", None, None),
        ),
        check_vma=False,
    )
```

profile of v0, /device:TPU:1, one launch (start us, length us, event | category | flops | bytes accessed | tf_op | source)
XLA Modules:
  0.0 150.3 jit_solution(10058551639044590301)
XLA Ops:
  7.3 0.8 broadcast_compare_fusion
  8.0 0.8 fusion.11
  8.8 0.8 copy.78
  9.7 0.8 copy.79
  10.6 1.0 copy.85
  11.6 22.7 %all_gather.16 = f32[512,256]{1,0:T(8,128)S(1)} all-gather(f32[32,256]{1,0:T(8,128)S(1)} %pad_maximum_fusion.2), channel_id=1, replica_groups=mesh['row'=16,'col'=16] {'col'}, dimensions={0}, use_global_device_ids=true | all-gather | bytes 557056 | tf_op jit(solution)/shard_map/all_gather | solution.py:10
  34.7 2.2 %broadcast_select_fusion.3 = (f32[64,256,1]{0,2,1:T(1,128)S(1)}, f32[64,256,1]{0,2,1:T(1,128)S(1)}) fusion(pred[256]{0:T(512)(128)(4,1)S(1)} %broadcast_compare_fusion, f32[64,256,2]{0,2,1:T(2,128)S(1)} %bitcast.108, f32[256]{0:T(256)S(1)} %bitcast.120, f32[256]{0:T(256)S(1)} %bitcast.126, f32[256]{0:T(256)S(1)} %bitcast.123, f32[256]{0:T(256)S(1)} %bitcast.117), kind=kLoop, calls=%fused_computation.11 | loop fusion | flops 196608 | bytes 266496 | tf_op jit(solution)/shard_map/jit(_where)/select_n | solution.py:31
  36.9 0.3 pad_maximum_fusion
  37.2 0.5 fusion.1
  37.7 0.4 fusion.14
  38.1 0.4 convolution_bitcast_fusion.1
  38.5 0.3 convolution_subtract_fusion
  38.8 1.1 convolution_bitcast_fusion
  40.4 19.9 %all_gather.15 = f32[512,256]{1,0:T(8,128)S(1)} all-gather(f32[32,256]{1,0:T(8,128)S(1)} %pad_maximum_fusion.1), channel_id=1, replica_groups=mesh['row'=16,'col'=16] {'row'}, dimensions={0}, use_global_device_ids=true | all-gather | bytes 557056 | tf_op jit(solution)/shard_map/all_gather | solution.py:10
  60.6 11.0 %copy.84 = f32[2,1,512,2,1,512]{2,5,0,3,4,1:T(8,128)} copy(f32[2,1,512,2,1,512]{5,4,3,2,1,0:T(1,128)} %param.12) | data formatting | bytes 8388608 | tf_op args[0]
  71.6 0.5 fusion.12
  72.1 0.6 fusion.13
  72.7 6.7 %bitcast_subtract_fusion = f32[2,1,512,2,1,512]{2,5,0,3,4,1:T(8,128)} fusion(f32[2,1,512,2,1,512]{2,5,0,3,4,1:T(8,128)} %copy.84, f32[2,64,512,1]{2,1,3,0:T(8,128)S(1)} %bitcast.109, f32[2,512,2,64]{1,3,0,2:T(8,128)S(1)} %fusion.13), kind=kOutput, calls=%fused_computation.1 | convolution fusion | flops 806354944 | bytes 9175040 | tf_op jit(solution)/shard_map/apbs,bsq->apbq/dot_general | solution.py:71
  79.4 10.9 %copy.91 = f32[2,1,512,2,1,512]{5,4,3,2,1,0:T(1,128)} copy(f32[2,1,512,2,1,512]{2,5,0,3,4,1:T(8,128)} %bitcast_subtract_fusion) | data formatting | bytes 8388608
  90.3 2.6 %reduce_sum.9 = f32[2,64,512]{2,1,0:T(8,128)S(1)} reduce(f32[16,2,64,512]{3,2,1,0:T(8,128)} %bitcast.101, f32[]{:T(128)} %constant.67.clone.1), dimensions={0}, to_apply=%region_0.1 | reduce | flops 983040 | bytes 4456452 | tf_op jit(solution)/shard_map/reduce_sum | solution.py:19
  93.0 0.4 fusion.15
  93.5 11.7 %custom-call.8 = f32[2,64,64]{2,1,0:T(8,128)S(1)} custom-call(f32[2,64,64]{2,1,0:T(8,128)S(1)} %fusion.7), custom_call_target="Cholesky" | custom-call | tf_op jit(solution)/shard_map/jit(cholesky)/cholesky | solution.py:83
  105.4 9.8 %custom-call.9 = f32[2,1,64,64]{2,3,1,0:T(8,128)S(1)} custom-call(f32[2,1,64,64]{3,2,1,0:T(8,128)S(1)} %select_bitcast_fusion), custom_call_target="InvertDiagBlocksLowerTriangular" | custom-call | tf_op jit(solution)/shard_map/vmap(jit(_solve_triangular))/triangular_solve | solution.py:41
  115.3 0.4 fusion.5
  115.7 0.3 fusion.16
  116.1 20.6 %all_gather.19 = f32[2,64,512]{1,2,0:T(8,128)S(1)} all-gather(f32[2,64,32]{1,2,0:T(8,128)S(1)} %fusion.16), channel_id=1, replica_groups=mesh['row'=16,'col'=16] {'col'}, dimensions={2}, use_global_device_ids=true | all-gather | bytes 278528 | tf_op jit(solution)/shard_map/all_gather | solution.py:85
  136.6 0.4 copy.89
  137.0 2.1 %gather_fusion = f32[512,2,64]{2,1,0:T(2,128)S(1)} fusion(f32[2,64,512]{1,0,2:T(2,128)S(1)} %copy.89, s32[1024]{0:T(1024)S(1)} %pad_clamp_fusion), kind=kCustom, calls=%fused_computation | custom fusion | bytes 526336 | tf_op jit(solution)/shard_map/jit(_take)/gather | solution.py:86
  139.1 0.6 copy_select_fusion
  139.8 2.2 %broadcast_select_fusion.1 = (f32[2,64,256,1]{1,3,2,0:T(1,128)S(1)}, f32[2,64,256,1]{1,3,2,0:T(1,128)S(1)}) fusion(pred[256]{0:T(512)(128)(4,1)S(1)} %broadcast_compare_fusion, f32[2,64,256,2]{1,3,2,0:T(2,128)S(1)} %copy_select_fusion, f32[256]{0:T(256)S(1)} %bitcast.122, f32[256]{0:T(256)S(1)} %multiply_subtract_fusion, f32[256]{0:T(256)S(1)} %bitcast.125, ...), kind=kLoop, calls=%fused_computation.8 | loop fusion | flops 393216 | bytes 528640 | tf_op jit(solution)/shard_map/jit(_where)/select_n | solution.py:31
  142.0 0.6 maximum_multiply_fusion
  142.6 0.9 copy.93
  (44 shorter events, 1.7 us)
Async XLA Ops:
  7.2 30.0 %copy-start = (f32[64,512]{1,0:T(8,128)S(1)}, f32[64,512]{1,0:T(8,128)}, u32[]{:S(2)}) copy-start(f32[64,512]{1,0:T(8,128)} %param.19) | copy-start | bytes 393220
  7.2 30.9 %copy-start.5 = (s32[512]{0:T(512)S(1)}, s32[512]{0:T(512)}, u32[]{:S(2)}) copy-start(s32[512]{0:T(512)} %param.21) | copy-start | bytes 6148
  7.2 31.3 %copy-start.6 = (f32[64,32]{0,1:T(8,128)S(1)}, f32[64,32]{0,1:T(8,128)}, u32[]{:S(2)}) copy-start(f32[64,32]{0,1:T(8,128)} %param.18) | copy-start | bytes 24580
  7.2 31.3 %copy-start.2 = (f32[2,1,512,32]{2,3,1,0:T(8,128)S(1)}, f32[2,1,512,32]{2,3,1,0:T(8,128)}, u32[]{:S(2)}) copy-start(f32[2,1,512,32]{2,3,1,0:T(8,128)} %param.13) | copy-start | bytes 393220
  7.2 33.0 %copy-start.3 = (f32[2,1,64,32]{2,3,1,0:T(8,128)S(1)}, f32[2,1,64,32]{2,3,1,0:T(8,128)}, u32[]{:S(2)}) copy-start(f32[2,1,64,32]{2,3,1,0:T(8,128)} %param.16) | copy-start | bytes 49156
  7.2 33.1 %copy-start.4 = (f32[2,1,64,32]{2,3,1,0:T(8,128)S(1)}, f32[2,1,64,32]{2,3,1,0:T(8,128)}, u32[]{:S(2)}) copy-start(f32[2,1,64,32]{2,3,1,0:T(8,128)} %param.17) | copy-start | bytes 49156
  7.2 83.1 %all-gather.3.cloned.1.call-start = ((), (), s32[]{:S(2)}) async-start(), calls=%async_computation | async-start | bytes 4456448 | tf_op jit(solution)/shard_map/all_gather | solution.py:19
  115.7 27.8 %copy-start.1 = (f32[2,64,512]{2,1,0:T(8,128)}, f32[2,64,512]{2,1,0:T(8,128)S(1)}, u32[]{:S(2)}) copy-start(f32[2,64,512]{2,1,0:T(8,128)S(1)} %fusion.5) | copy-start | bytes 786436
Sparse Core Ops, SparseCore 0:
  40.1 40.0 all-gather.2
where the time goes:
time: 151 us; the launch traced here: 150 us
  blocking collectives  63.2 us (42%)
  other arithmetic  32 us (21%)
  local copies, waits for them, and re-layouts  29.1 us (19%)
  between operations  14.4 us (10%)
  matrix products  11.7 us (8%)
    all_gather x2, blocking collectives, gather_turned(): filled, at, outs = (lax.all_gather(both, axis, axis=0, tiled=True), 0, [])  42.6 us
    unnamed x18, local copies, waits for them, and re-layouts  23.8 us
    all_gather x1, blocking collectives, body(): projected = lax.all_gather(projected_part, 'col', axis=2, tiled=True)  20.6 us
    another operation x4, other arithmetic, body(): basis = tri_solve(jnp.linalg.cholesky(gram), range_t)  11.9 us
    another operation x3, other arithmetic, tri_solve(): jax.scipy.linalg.solve_triangular(low, right, lower=True)  9.92 us
    dot_general x1, matrix products, body(): change = jnp.einsum('apbs,bsq->apbq', left, zcols, precision=highest)  6.7 us
    select_n x2, other arithmetic, pair_apply(): jnp.where(twin, (first_in * diag_two - second_in * offdiag) / determinant...  4.37 us
  transfers between devices with their start and end apart: 1, of which 0 were waited for; matrix products, arithmetic and copies ran while one was open for 20% of the time, Pallas kernels for 0%

commit v1 on v0

--- a/solution.py
+++ b/solution.py
@@ -4,10 +4,17 @@
 from jax.sharding import PartitionSpec as P
 
 
+def exchange_gather(x, name, d):
+    size = lax.axis_size(name)
+    tiles = jnp.stack([x for _ in range(size)])
+    tiles = lax.all_to_all(tiles, name, split_axis=0, concat_axis=0)
+    return jnp.concatenate(tiles, axis=d)
+
+
 def gather_turned(arrays, axis, dims):
     turned = [jnp.moveaxis(a, dim, 0) for a, dim in zip(arrays, dims)]
     both = jnp.concatenate([t.reshape(len(t), -1) for t in turned], axis=1)
-    filled, at, outs = (lax.all_gather(both, axis, axis=0, tiled=True), 0, [])
+    filled, at, outs = (exchange_gather(both, axis, 0), 0, [])
     for t, dim in zip(turned, dims):
         share = filled[:, at : at + t[0].size].reshape(-1, *t.shape[1:])
         outs.append(jnp.moveaxis(share, 0, dim))

time: 151 us -> 137 us (0.907)
  blocking collectives: 63.2 us -> 17.8 us
  starting transfers between devices: 0.04 us -> 16.8 us
  waiting for transfers between devices: 0.04 us -> 12.3 us
  local copies, waits for them, and re-layouts: 29.1 us -> 30.9 us
    all_gather x2 -> x0, blocking collectives: 42.6 us -> none  [gather_turned(): filled, at, outs = (lax.all_gather(both, axis, axis=0, tiled=True), 0, [])]
    all_to_all x0 -> x2, starting transfers between devices: none -> 16.7 us  [exchange_gather(): tiles = lax.all_to_all(tiles, name, split_axis=0, concat_axis=0)]
    all_to_all x0 -> x2, waiting for transfers between devices: none -> 11.2 us  [exchange_gather(): tiles = lax.all_to_all(tiles, name, split_axis=0, concat_axis=0)]
    all_gather x1, blocking collectives: 20.6 us -> 17.8 us  [body(): projected = lax.all_gather(projected_part, 'col', axis=2, tiled=True)]
    another operation x0 -> x2, local copies, waits for them, and re-layouts: none -> 1.7 us  [exchange_gather(): tiles = jnp.stack([x for _ in range(size)])]
  transfers between devices with their start and end apart: 1 -> 3, of which waited for: 0 -> 3; matrix products, arithmetic and copies ran while one was open for 20% -> 27% of each run, Pallas kernels for 0% -> 0%
where the time goes in v1:
time: 137 us; the launch traced here: 136 us
  other arithmetic  31.9 us (23%)
  local copies, waits for them, and re-layouts  30.9 us (23%)
  blocking collectives  17.8 us (13%)
  starting transfers between devices  16.8 us (12%)
  between operations  14.4 us (11%)
  matrix products  12.3 us (9%)
  waiting for transfers between devices  12.3 us (9%)
    unnamed x18, local copies, waits for them, and re-layouts  23.8 us
    all_gather x1, blocking collectives, body(): projected = lax.all_gather(projected_part, 'col', axis=2, tiled=True)  17.8 us
    all_to_all x2, starting transfers between devices, exchange_gather(): tiles = lax.all_to_all(tiles, name, split_axis=0, concat_axis=0)  16.7 us
    another operation x4, other arithmetic, body(): basis = tri_solve(jnp.linalg.cholesky(gram), range_t)  11.9 us
    all_to_all x2, waiting for transfers between devices, exchange_gather(): tiles = lax.all_to_all(tiles, name, split_axis=0, concat_axis=0)  11.2 us
    another operation x3, other arithmetic, tri_solve(): jax.scipy.linalg.solve_triangular(low, right, lower=True)  9.92 us
    dot_general x1, matrix products, body(): change = jnp.einsum('apbs,bsq->apbq', left, zcols, precision=highest)  6.69 us
    select_n x2, other arithmetic, pair_apply(): jnp.where(twin, (first_in * diag_two - second_in * offdiag) / determinant...  4.34 us
  transfers between devices with their start and end apart: 3, of which 3 were waited for; matrix products, arithmetic and copies ran while one was open for 27% of the time, Pallas kernels for 0%

profile of v1, /device:TPU:1, one launch (start us, length us, event | category | flops | bytes accessed | tf_op | source)
XLA Modules:
  0.0 136.3 jit_solution(15535889499877135781)
XLA Ops:
  7.2 0.9 copy.77
  8.2 0.8 copy.78
  9.1 0.8 stack.9
  9.9 10.0 %all-to-all-start.1 = ((f32[16,32,256]{2,1,0:T(8,128)}), f32[16,32,256]{2,1,0:T(8,128)S(1)}, u32[]{:S(2)}, u32[]{:S(2)}) async-start(f32[16,32,256]{2,1,0:T(8,128)} %stack.9), calls=%async_computation.1 | async-start | bytes 1048576 | tf_op jit(solution)/shard_map/all_to_all | solution.py:10
  19.9 0.8 fusion.11
  20.8 1.0 copy.84
  21.8 0.7 broadcast_compare_fusion
  22.5 2.1 %broadcast_select_fusion.3 = (f32[64,256,1]{0,2,1:T(1,128)S(1)}, f32[64,256,1]{0,2,1:T(1,128)S(1)}) fusion(pred[256]{0:T(512)(128)(4,1)S(1)} %broadcast_compare_fusion, f32[64,256,2]{0,2,1:T(2,128)S(1)} %bitcast.113, f32[256]{0:T(256)S(1)} %bitcast.124, f32[256]{0:T(256)S(1)} %bitcast.130, f32[256]{0:T(256)S(1)} %bitcast.127, f32[256]{0:T(256)S(1)} %bitcast.121), kind=kLoop, calls=%fused_computation.11 | loop fusion | flops 196608 | bytes 266496 | tf_op jit(solution)/shard_map/jit(_where)/select_n | solution.py:38
  24.9 1.1 convolution_bitcast_fusion.1
  26.1 11.0 %all-to-all-done.1 = f32[16,32,256]{2,1,0:T(8,128)S(1)} async-done(((f32[16,32,256]{2,1,0:T(8,128)}), f32[16,32,256]{2,1,0:T(8,128)S(1)}, u32[]{:S(2)}, u32[]{:S(2)}) %all-to-all-start.1) | async-done | bytes 524320 | tf_op jit(solution)/shard_map/all_to_all | solution.py:10
  37.4 0.5 fusion.1
  37.9 0.4 fusion.14
  38.6 1.1 convolution_bitcast_fusion
  40.0 0.9 stack.8
  40.9 6.8 %all-to-all-start = ((f32[16,32,256]{2,1,0:T(8,128)}), f32[16,32,256]{2,1,0:T(8,128)S(1)}, u32[]{:S(2)}, u32[]{:S(2)}) async-start(f32[16,32,256]{2,1,0:T(8,128)} %stack.8), calls=%async_computation | async-start | bytes 1048576 | tf_op jit(solution)/shard_map/all_to_all | solution.py:10
  47.9 10.9 %copy.83 = f32[2,1,512,2,1,512]{2,5,0,3,4,1:T(8,128)} copy(f32[2,1,512,2,1,512]{5,4,3,2,1,0:T(1,128)} %param.12) | data formatting | bytes 8388608 | tf_op args[0]
  59.3 0.5 fusion.12
  59.8 0.6 fusion.13
  60.4 6.7 %bitcast_subtract_fusion = f32[2,1,512,2,1,512]{2,5,0,3,4,1:T(8,128)} fusion(f32[2,1,512,2,1,512]{2,5,0,3,4,1:T(8,128)} %copy.83, f32[2,64,512,1]{2,1,3,0:T(8,128)S(1)} %bitcast.112, f32[2,512,2,64]{1,3,0,2:T(8,128)S(1)} %fusion.13), kind=kOutput, calls=%fused_computation.1 | convolution fusion | flops 806354944 | bytes 9175040 | tf_op jit(solution)/shard_map/apbs,bsq->apbq/dot_general | solution.py:78
  67.1 10.9 %copy.90 = f32[2,1,512,2,1,512]{5,4,3,2,1,0:T(1,128)} copy(f32[2,1,512,2,1,512]{2,5,0,3,4,1:T(8,128)} %bitcast_subtract_fusion) | data formatting | bytes 8388608
  78.0 1.0 all-gather.3.cloned.1.call-done
  79.1 2.6 %reduce_sum.9 = f32[2,64,512]{2,1,0:T(8,128)S(1)} reduce(f32[16,2,64,512]{3,2,1,0:T(8,128)} %bitcast.103, f32[]{:T(128)} %constant.67.clone.1), dimensions={0}, to_apply=%region_0.1 | reduce | flops 983040 | bytes 4456452 | tf_op jit(solution)/shard_map/reduce_sum | solution.py:26
  82.2 11.7 %custom-call.8 = f32[2,64,64]{2,1,0:T(8,128)S(1)} custom-call(f32[2,64,64]{2,1,0:T(8,128)S(1)} %fusion.7), custom_call_target="Cholesky" | custom-call | tf_op jit(solution)/shard_map/jit(cholesky)/cholesky | solution.py:90
  94.2 9.8 %custom-call.9 = f32[2,1,64,64]{2,3,1,0:T(8,128)S(1)} custom-call(f32[2,1,64,64]{3,2,1,0:T(8,128)S(1)} %select_bitcast_fusion), custom_call_target="InvertDiagBlocksLowerTriangular" | custom-call | tf_op jit(solution)/shard_map/vmap(jit(_solve_triangular))/triangular_solve | solution.py:48
  104.0 0.4 fusion.5
  104.8 17.8 %all_gather.11 = f32[2,64,512]{1,2,0:T(8,128)S(1)} all-gather(f32[2,64,32]{1,2,0:T(8,128)S(1)} %fusion.16), channel_id=1, replica_groups=mesh['row'=16,'col'=16] {'col'}, dimensions={2}, use_global_device_ids=true | all-gather | bytes 278528 | tf_op jit(solution)/shard_map/all_gather | solution.py:92
  122.6 0.4 copy.88
  123.0 2.1 %gather_fusion = f32[512,2,64]{2,1,0:T(2,128)S(1)} fusion(f32[2,64,512]{1,0,2:T(2,128)S(1)} %copy.88, s32[1024]{0:T(1024)S(1)} %pad_clamp_fusion), kind=kCustom, calls=%fused_computation | custom fusion | bytes 526336 | tf_op jit(solution)/shard_map/jit(_take)/gather | solution.py:93
  125.1 0.6 copy_select_fusion
  125.7 2.2 %broadcast_select_fusion.1 = (f32[2,64,256,1]{1,3,2,0:T(1,128)S(1)}, f32[2,64,256,1]{1,3,2,0:T(1,128)S(1)}) fusion(pred[256]{0:T(512)(128)(4,1)S(1)} %broadcast_compare_fusion, f32[2,64,256,2]{1,3,2,0:T(2,128)S(1)} %copy_select_fusion, f32[256]{0:T(256)S(1)} %bitcast.126, f32[256]{0:T(256)S(1)} %multiply_subtract_fusion, f32[256]{0:T(256)S(1)} %bitcast.129, ...), kind=kLoop, calls=%fused_computation.8 | loop fusion | flops 393216 | bytes 528640 | tf_op jit(solution)/shard_map/jit(_where)/select_n | solution.py:38
  127.9 0.6 maximum_multiply_fusion
  128.6 0.9 copy.92
  (48 shorter events, 3.1 us)
Async XLA Ops:
  7.2 30.2 %copy-start = (f32[64,512]{1,0:T(8,128)S(1)}, f32[64,512]{1,0:T(8,128)}, u32[]{:S(2)}) copy-start(f32[64,512]{1,0:T(8,128)} %param.19) | copy-start | bytes 393220
  7.2 31.1 %copy-start.6 = (f32[64,32]{0,1:T(8,128)S(1)}, f32[64,32]{0,1:T(8,128)}, u32[]{:S(2)}) copy-start(f32[64,32]{0,1:T(8,128)} %param.18) | copy-start | bytes 24580
  7.2 31.1 %copy-start.2 = (f32[2,1,512,32]{2,3,1,0:T(8,128)S(1)}, f32[2,1,512,32]{2,3,1,0:T(8,128)}, u32[]{:S(2)}) copy-start(f32[2,1,512,32]{2,3,1,0:T(8,128)} %param.13) | copy-start | bytes 393220
  7.2 32.5 %copy-start.3 = (f32[2,1,64,32]{2,3,1,0:T(8,128)S(1)}, f32[2,1,64,32]{2,3,1,0:T(8,128)}, u32[]{:S(2)}) copy-start(f32[2,1,64,32]{2,3,1,0:T(8,128)} %param.16) | copy-start | bytes 49156
  7.2 32.7 %copy-start.4 = (f32[2,1,64,32]{2,3,1,0:T(8,128)S(1)}, f32[2,1,64,32]{2,3,1,0:T(8,128)}, u32[]{:S(2)}) copy-start(f32[2,1,64,32]{2,3,1,0:T(8,128)} %param.17) | copy-start | bytes 49156
  9.9 27.2 %all-to-all-start.1 = ((f32[16,32,256]{2,1,0:T(8,128)}), f32[16,32,256]{2,1,0:T(8,128)S(1)}, u32[]{:S(2)}, u32[]{:S(2)}) async-start(f32[16,32,256]{2,1,0:T(8,128)} %stack.9), calls=%async_computation.1 | async-start | bytes 1048576 | tf_op jit(solution)/shard_map/all_to_all | solution.py:10
  19.9 27.8 %copy-start.5 = (s32[512]{0:T(512)S(1)}, s32[512]{0:T(512)}, u32[]{:S(2)}) copy-start(s32[512]{0:T(512)} %param.21) | copy-start | bytes 6148
  19.9 59.2 %all-gather.3.cloned.1.call-start = ((), (), s32[]{:S(2)}) async-start(), calls=%async_computation.2 | async-start | bytes 4456448 | tf_op jit(solution)/shard_map/all_gather | solution.py:26
  40.9 18.1 %all-to-all-start = ((f32[16,32,256]{2,1,0:T(8,128)}), f32[16,32,256]{2,1,0:T(8,128)S(1)}, u32[]{:S(2)}, u32[]{:S(2)}) async-start(f32[16,32,256]{2,1,0:T(8,128)} %stack.8), calls=%async_computation | async-start | bytes 1048576 | tf_op jit(solution)/shard_map/all_to_all | solution.py:10
  104.4 25.0 %copy-start.1 = (f32[2,64,512]{2,1,0:T(8,128)}, f32[2,64,512]{2,1,0:T(8,128)S(1)}, u32[]{:S(2)}) copy-start(f32[2,64,512]{2,1,0:T(8,128)S(1)} %fusion.5) | copy-start | bytes 786436
Sparse Core Ops, SparseCore 0:
  39.9 39.1 all-gather.2
